TPU v7x, 32 devices: a whole 2x2x4 slice. The times are simulated.
32 devices in a mesh: sub: 16 (over z, x, core), sec: 2 (over y).
Axes of the slice: x: 2, y: 2, z: 4, core: 2. Of those that a mesh axis runs over, the one named last changes fastest.
Arguments:
- image: bfloat16 [16, 2, 512, 512], P('sub', None, 'sec'), may hold values from -6 to 6
- range_offsets: int32 [16, 3, 2, 4], P('sub'), may hold values from 0 to 16
- tap_weights: bfloat16 [16, 3, 2, 128, 8], P('sub'), may hold values from -1.1953125 to 1.1953125
- beam_weights: float32 [16, 3, 2, 4], P('sub'), may hold values from 0.25 to 1
- phase_rates: float32 [16, 3, 2], P('sub'), may hold values from 1 to 40
Outputs:
- merged: bfloat16 [16, 2, 512, 512], P('sub', None, 'sec')
All inputs are finite; a program needn't handle non-finite values.
Results may differ from a plain program's by a relative error of at most 0.0043.
Values may be sent and summed in bfloat16 or wider, within the bound.
A program may use at most 64 MiB of HBM per device.

v0:
```python
import functools
import math

import jax
import jax.numpy as jnp
from jax import lax
from jax.experimental import pallas as pl
from jax.experimental.pallas import tpu as pltpu
from jax.sharding import PartitionSpec as P

SECTIONS = 3
BLOCK = 128
TAPS = 8
MARGIN_ROWS = 12
TILE = 16
STEP = 2
LAG = 3
MESH = pl.DeviceIdType.MESH


def bounds(tiles):
    inner = list(range(2, tiles - 1, STEP)) + [tiles - 1]
    first = [0] + [v + 1 for v in inner] + [tiles + 1]
    second = [0] + inner + [tiles + 1]
    third = [0] + [v - 1 for v in inner] + [tiles]
    return first, second, third


def sincos_turns(turns):
    x = (turns - jnp.round(turns)) * math.pi
    y = x * x
    s = -1.0 / math.factorial(11)
    for n in (9, 7, 5, 3, 1):
        s = s * y + (1.0 if n % 4 == 1 else -1.0) / math.factorial(n)
    s = s * x
    c = 1.0 / math.factorial(12)
    for n in (10, 8, 6, 4, 2, 0):
        c = c * y + (1.0 if n % 4 == 0 else -1.0) / math.factorial(n)
    return 1.0 - 2.0 * s * s, 2.0 * s * c


def kernel(n_sec, chunks, image_hbm, offsets_hbm, taps_hbm, weights_hbm, rates_hbm, out,
           image, offsets, taps, weights, rates, load_sem, recv0, halo_own, halo_far, s1, r1, s2, r2, band, q, fine, coarse,
           send_sem, recv_sem, hsend_sem, hrecv_sem):
    sub = lax.axis_index("sub")
    sec = lax.axis_index("sec")
    beams, range_len = image.shape[2], image.shape[3]
    tiles = beams // TILE
    blocks = range_len // BLOCK
    partners = []
    for k in range(SECTIONS):
        bit = 1 << k
        partners.append(sub + bit * (1 - 2 * ((sub // bit) % 2)))
    has_low = sec > 0
    has_high = sec < n_sec - 1

    loads = [pltpu.make_async_copy(src, dst, load_sem.at[n]) for n, (src, dst) in enumerate((
        (image_hbm, image), (offsets_hbm, offsets), (taps_hbm, taps), (weights_hbm, weights), (rates_hbm, rates)))]
    for load in loads:
        load.start()

    barrier = pltpu.get_barrier_semaphore()
    for k in range(SECTIONS):
        pl.semaphore_signal(barrier, inc=1, device_id={"sub": partners[k]}, device_id_type=MESH)
    for cond, step in ((has_low, -1), (has_high, 1)):
        @pl.when(cond)
        def _():
            for dst in (sub, partners[0]):
                pl.semaphore_signal(barrier, inc=1, device_id={"sub": dst, "sec": sec + step}, device_id_type=MESH)
    sectors_beside = (sec + n_sec - 1) // n_sec + (2 * (n_sec - 1) - sec) // n_sec
    for k in range(1, SECTIONS):
        for child in range(2):
            for z in range(2):
                for n in range(blocks):
                    q[k, child, z, n, 0:8, :] = jnp.zeros((8, BLOCK), jnp.float32)
                    q[k, child, z, n, beams + 24:beams + 32, :] = jnp.zeros((8, BLOCK), jnp.float32)
    loads[0].wait()
    pl.semaphore_wait(barrier, SECTIONS + 2 * sectors_beside)

    b1, b2, b3 = bounds(tiles)
    outs = (b1, b2, b3)
    ins = ([0] + [v + 1 for v in b1[1:]], b1, b2)

    def halo_copy(side, far):
        rows = pl.ds(beams - TILE, TILE) if side == 0 else pl.ds(0, TILE)
        dst = halo_far if far else halo_own
        return pltpu.make_async_remote_copy(
            src_ref=image.at[0, :, rows, :], dst_ref=dst.at[side],
            send_sem=hsend_sem.at[side, far], recv_sem=hrecv_sem.at[side, far],
            device_id={"sub": partners[0] if far else sub, "sec": sec + (1 if side == 0 else -1)},
            device_id_type=MESH)

    def span(k, j):
        lo, hi = ins[k][j], ins[k][j + 1]
        if k == 0:
            lo, hi = max(lo - 1, 0), min(hi - 1, tiles)
        return lo * TILE, (hi - lo) * TILE

    sources = ((image.at[0], recv0), (s1, r1), (s2, r2))

    def main_copy(k, j):
        lo, size = span(k, j)
        src, dst = sources[k]
        return pltpu.make_async_remote_copy(
            src_ref=src.at[:, pl.ds(lo, size), :], dst_ref=dst.at[:, pl.ds(lo, size), :],
            send_sem=send_sem.at[k, j], recv_sem=recv_sem.at[k, j],
            device_id={"sub": partners[k]}, device_id_type=MESH)

    for side, cond in ((0, has_high), (1, has_low)):
        @pl.when(cond)
        def _():
            for far in (1, 0):
                halo_copy(side, far).start()
    live = [[j for j in range(chunks) if span(k, j)[1]] for k in range(SECTIONS)]
    for j in live[0]:
        main_copy(0, j).start()
    for side, cond in ((0, has_low), (1, has_high)):
        @pl.when(jnp.logical_not(cond))
        def _():
            halo_own[side] = jnp.zeros(halo_own.shape[1:], halo_own.dtype)
            halo_far[side] = jnp.zeros(halo_far.shape[1:], halo_far.dtype)

    sector_start = sec * beams
    total_beams = beams * n_sec

    def prepare(k):
        base = 0 if k == SECTIONS - 1 else -8
        for child in range(2):
            tap = taps[0, k, child].astype(jnp.float32)
            for n in range(blocks):
                lo = max(n * BLOCK - 16, 0)
                hi = min((n + 1) * BLOCK + 16, range_len)
                cols = slice(n * BLOCK, (n + 1) * BLOCK)
                if lo > 0:
                    band[k, child, 0:lo, cols] = jnp.zeros((lo, BLOCK), jnp.bfloat16)
                if hi < range_len:
                    band[k, child, hi:range_len, cols] = jnp.zeros((range_len - hi, BLOCK), jnp.bfloat16)
                which = (lax.broadcasted_iota(jnp.int32, (hi - lo, BLOCK), 0)
                         - lax.broadcasted_iota(jnp.int32, (hi - lo, BLOCK), 1)
                         + (lo - n * BLOCK + MARGIN_ROWS)) - offsets[0, k, child, n]
                value = jnp.zeros((hi - lo, BLOCK), jnp.float32)
                for t in range(TAPS):
                    value = jnp.where(which == t, tap[t:t + 1, :], value)
                band[k, child, lo:hi, cols] = value.astype(jnp.bfloat16)
            per_turn = rates[0, child, k] * (1.0 / (2.0 * math.pi * range_len * total_beams))
            for ref, first, scale in ((fine, sector_start + base + 1, 1), (coarse, 0, TILE)):
                shape = ref.shape[4:]
                beam = (first + scale * lax.broadcasted_iota(jnp.int32, shape, 0)).astype(jnp.float32)
                for n in range(blocks):
                    rng = (lax.broadcasted_iota(jnp.int32, shape, 1) + (n * BLOCK + 1)).astype(jnp.float32)
                    c, s = sincos_turns(beam * rng * per_turn)
                    ref[k, child, 0, n] = c
                    ref[k, child, 1, n] = s

    def interpolate(k, child, data, row):
        rows = data.shape[1]
        flat = data.reshape(2 * rows, range_len)
        for at in range(0, blocks, 2):
            end = min(at + 2, blocks)
            lo, hi = max(at - 1, 0) * BLOCK, min(end + 1, blocks) * BLOCK
            res = jnp.dot(flat[:, lo:hi], band[k, child, lo:hi, at * BLOCK:end * BLOCK],
                          preferred_element_type=jnp.float32)
            for z in range(2):
                for n in range(at, end):
                    q[k, child, z, n, row:row + rows, :] = res[z * rows:(z + 1) * rows, (n - at) * BLOCK:(n - at + 1) * BLOCK]

    def interpolate_chunk(k, child, j):
        ref = sources[k][child]
        lo, size = span(k, j)
        if k == 0:
            halo = halo_own if child == 0 else halo_far
            if j == 0:
                interpolate(k, child, halo[0], 0)
            if size and child == 1:
                interpolate(k, child, ref[:, lo:lo + size, :], lo + TILE)
            if j == chunks - 1:
                interpolate(k, child, halo[1], beams + TILE)
        else:
            interpolate(k, child, ref[:, lo:lo + size, :], lo + 8)

    def combine(k, j):
        base = 0 if k == SECTIONS - 1 else -8
        bw = [[weights[0, k, child, a] for a in range(4)] for child in range(2)]
        first, last = outs[k][j], outs[k][j + 1]

        def tile(t, carry):
            row = pl.multiple_of(t * TILE, TILE)
            view = q.at[k, :, :, :, pl.ds(pl.multiple_of(row + (base + 8), 8), 2 * TILE), :]
            if k < SECTIONS - 1:
                beam = sector_start + base + row + lax.broadcasted_iota(jnp.int32, (TILE, BLOCK), 0)
                inside = (beam >= 0) & (beam < total_beams)
            for n in range(blocks):
                cols = slice(n * BLOCK, (n + 1) * BLOCK)
                total = [None, None]
                for child in range(2):
                    g = []
                    for z in range(2):
                        acc = None
                        for a in range(4):
                            term = bw[child][a] * view[child, z, n, 7 + a:7 + a + TILE, :]
                            acc = term if acc is None else acc + term
                        g.append(acc)
                    cc = coarse[k, child, 0, n, pl.ds(t, 1), :]
                    cs = coarse[k, child, 1, n, pl.ds(t, 1), :]
                    fc = fine[k, child, 0, n]
                    fs = fine[k, child, 1, n]
                    cosine = cc * fc - cs * fs
                    sine = cs * fc + cc * fs
                    re = cosine * g[0] - sine * g[1]
                    im = sine * g[0] + cosine * g[1]
                    total = [re, im] if child == 0 else [total[0] + re, total[1] + im]
                for z in range(2):
                    v = total[z]
                    if k < SECTIONS - 1:
                        v = jnp.where(inside, v, 0.0)
                        (s1, s2)[k][z, pl.ds(row, TILE), cols] = v.astype(jnp.bfloat16)
                    else:
                        out[0, z, pl.ds(row, TILE), cols] = v.astype(jnp.bfloat16)
            return carry

        lax.fori_loop(first, last, tile, 0)

    def step(k, j):
        if k == 0:
            for side, at, cond in ((0, 0, has_low), (1, chunks - 1, has_high)):
                if j == at:
                    @pl.when(cond)
                    def _():
                        for far in (1, 0):
                            halo_copy(side, far).wait_recv()
        if k == 0:
            interpolate_chunk(k, 0, j)
        if j in live[k]:
            main_copy(k, j).wait_recv()
        interpolate_chunk(k, 1, j)
        combine(k, j)
        if k < SECTIONS - 1:
            main_copy(k + 1, j).start()
            if k > 0:
                interpolate_chunk(k + 1, 0, j)

    for load in loads[1:]:
        load.wait()
    prepare(0)
    interpolate(0, 0, image[0], TILE)
    step(0, 0)
    step(0, 1)
    prepare(1)
    for j in range(2, chunks):
        step(0, j)
    interpolate(1, 0, s1[...], 8)
    prepare(2)
    lag = LAG
    for j in range(chunks + lag):
        if j < chunks:
            step(1, j)
        if j >= lag:
            step(2, j - lag)

    for k in range(SECTIONS):
        for j in live[k]:
            main_copy(k, j).wait_send()
    for side, cond in ((0, has_high), (1, has_low)):
        @pl.when(cond)
        def _():
            for far in (1, 0):
                halo_copy(side, far).wait_send()


def solution(mesh):
    n_sec = mesh.shape["sec"]
    def body(image, range_offsets, tap_weights, beam_weights, phase_rates):
        _, _, beams, range_len = image.shape
        chunks = len(bounds(beams // TILE)[0]) - 1
        wide = beams + TILE
        rows = beams + 2 * TILE
        vmem = pl.BlockSpec(memory_space=pltpu.VMEM)
        taps = jnp.swapaxes(tap_weights, 3, 4)
        rates = jnp.swapaxes(phase_rates, 1, 2)
        coarse_rows = -(-(wide // TILE) // 8) * 8
        return pl.pallas_call(
            functools.partial(kernel, n_sec, chunks),
            out_shape=jax.ShapeDtypeStruct(image.shape, image.dtype),
            in_specs=[pl.BlockSpec(memory_space=pltpu.HBM)] * 5,
            out_specs=vmem,
            scratch_shapes=[
                pltpu.VMEM(image.shape, image.dtype),
                pltpu.SMEM(range_offsets.shape, range_offsets.dtype),
                pltpu.VMEM(taps.shape, taps.dtype),
                pltpu.SMEM(beam_weights.shape, beam_weights.dtype),
                pltpu.SMEM(rates.shape, rates.dtype),
                pltpu.SemaphoreType.DMA((5,)),
                pltpu.VMEM((2, beams, range_len), jnp.bfloat16),
                pltpu.VMEM((2, 2, TILE, range_len), jnp.bfloat16),
                pltpu.VMEM((2, 2, TILE, range_len), jnp.bfloat16),
                pltpu.VMEM((2, wide, range_len), jnp.bfloat16),
                pltpu.VMEM((2, wide, range_len), jnp.bfloat16),
                pltpu.VMEM((2, wide, range_len), jnp.bfloat16),
                pltpu.VMEM((2, wide, range_len), jnp.bfloat16),
                pltpu.VMEM((SECTIONS, 2, range_len, range_len), jnp.bfloat16),
                pltpu.VMEM((SECTIONS, 2, 2, range_len // BLOCK, rows, BLOCK), jnp.float32),
                pltpu.VMEM((SECTIONS, 2, 2, range_len // BLOCK, TILE, BLOCK), jnp.float32),
                pltpu.VMEM((SECTIONS, 2, 2, range_len // BLOCK, coarse_rows, BLOCK), jnp.float32),
                pltpu.SemaphoreType.DMA((SECTIONS, chunks)),
                pltpu.SemaphoreType.DMA((SECTIONS, chunks)),
                pltpu.SemaphoreType.DMA((2, 2)),
                pltpu.SemaphoreType.DMA((2, 2)),
            ],
            compiler_params=pltpu.CompilerParams(
                collective_id=0, has_side_effects=True),
        )(image, range_offsets, taps, beam_weights, rates)

    in_specs = (
        P("sub", None, "sec", None),
        P("sub", None, None, None),
        P("sub", None, None, None, None),
        P("sub", None, None, None),
        P("sub", None, None),
    )
    return jax.shard_map(body, mesh=mesh, in_specs=in_specs,
                         out_specs=P("sub", None, "sec", None), check_vma=False)
```

profile of v0, /device:TPU:0, one launch (start us, length us, event | category | flops | bytes accessed | tf_op | source)
XLA Modules:
  0.0 27.9 jit_solution(5683921008746293109)
XLA Ops:
  0.0 26.0 %shard_map.55 = bf16[1,2,256,512]{3,2,1,0:T(8,128)(2,1)} custom-call(bf16[1,2,256,512]{3,2,1,0:T(8,128)(2,1)} %image_hbm.1, s32[1,3,2,4]{3,2,1,0:T(2,128)} %offsets_hbm.1, bf16[1,3,2,8,128]{4,3,2,1,0:T(8,128)(2,1)} %bitcast.2, f32[1,3,2,4]{3,2,1,0:T(2,128)} %weights_hbm.1, f32[1,2,3]{2,1,0:T(2,128)} %bitcast.3), custom_call_target="tpu_custom_call" | custom-call | tf_op jit(solution)/shard_map/pallas_call | solution.py:281
  26.0 1.9 %copy.7 = bf16[1,2,256,512]{3,2,1,0:T(8,128)(2,1)} copy(bf16[1,2,256,512]{3,2,1,0:T(8,128)(2,1)} %shard_map.55) | data formatting | bytes 1048576
where the time goes:
time: 28.1 us; the launch traced here: 27.9 us
  Pallas kernels  26 us (93%)
  local copies, waits for them, and re-layouts  1.87 us (7%)
    pallas_call x1, Pallas kernels, body(): pl.pallas_call(functools.partial(kernel, n_sec, chunks), out_shape=jax.Sh...  26 us
    unnamed x1, local copies, waits for them, and re-layouts  1.87 us

commit v1 on v0

--- a/solution.py
+++ b/solution.py
@@ -280,7 +280,7 @@
         coarse_rows = -(-(wide // TILE) // 8) * 8
         return pl.pallas_call(
             functools.partial(kernel, n_sec, chunks),
-            out_shape=jax.ShapeDtypeStruct(image.shape, image.dtype),
+            out_shape=pltpu.VMEM(image.shape, image.dtype),
             in_specs=[pl.BlockSpec(memory_space=pltpu.HBM)] * 5,
             out_specs=vmem,
             scratch_shapes=[

time: 28.1 us -> 26.2 us (0.932)
  local copies, waits for them, and re-layouts: 1.87 us -> 0.8 us
  Pallas kernels: 26 us -> 25.2 us
    unnamed x1, local copies, waits for them, and re-layouts: 1.87 us -> 0.8 us
    pallas_call x1, Pallas kernels: 26 us -> 25.2 us  [body(): pl.pallas_call(functools.partial(kernel, n_sec, chunks), out_shape=pltpu....]
where the time goes in v1:
time: 26.2 us; the launch traced here: 26 us
  Pallas kernels  25.2 us (96%)
  local copies, waits for them, and re-layouts  0.8 us (3%)
    pallas_call x1, Pallas kernels, body(): pl.pallas_call(functools.partial(kernel, n_sec, chunks), out_shape=pltpu....  25.2 us
    unnamed x1, local copies, waits for them, and re-layouts  0.8 us

profile of v1, /device:TPU:0, one launch (start us, length us, event | category | flops | bytes accessed | tf_op | source)
XLA Modules:
  0.0 26.0 jit_solution(13552884182135421419)
XLA Ops:
  0.0 25.2 %shard_map.55 = bf16[1,2,256,512]{3,2,1,0:T(8,128)(2,1)S(1)} custom-call(bf16[1,2,256,512]{3,2,1,0:T(8,128)(2,1)} %image_hbm.1, s32[1,3,2,4]{3,2,1,0:T(2,128)} %offsets_hbm.1, bf16[1,3,2,8,128]{4,3,2,1,0:T(8,128)(2,1)} %bitcast.2, f32[1,3,2,4]{3,2,1,0:T(2,128)} %weights_hbm.1, f32[1,2,3]{2,1,0:T(2,128)} %bitcast.3), custom_call_target="tpu_custom_call" | custom-call | tf_op jit(solution)/shard_map/pallas_call | solution.py:281
  25.2 0.8 %copy.7 = bf16[1,2,256,512]{3,2,1,0:T(8,128)(2,1)} copy(bf16[1,2,256,512]{3,2,1,0:T(8,128)(2,1)S(1)} %shard_map.55) | data formatting | bytes 1048576
